TPU v7x, 32 devices: a whole 2x2x4 slice. The times are simulated.
32 devices in a mesh: rep: 2 (over x), model: 4 (over z), vocab: 4 (over y, core).
Axes of the slice: x: 2, y: 2, z: 4, core: 2. Of those that a mesh axis runs over, the one named last changes fastest.
Arguments:
- hidden: bfloat16 [1024, 3072], P(('rep', 'model', 'vocab')), parts along dimension 0
- head_rows: bfloat16 [128256, 3072], P(('model', 'vocab'))
- allowed_ids: int32 [1024, 64], P(('rep', 'model', 'vocab')), parts along dimension 0
- valid_mask: int32 [1024, 64], P(('rep', 'model', 'vocab')), parts along dimension 0
- target_pos: int32 [1024], P(('rep', 'model', 'vocab')), parts along dimension 0
Outputs:
- output 1: float32 [1024, 64], P(('rep', 'model', 'vocab')), parts along dimension 0
- output 2: float32 [1024], P(('rep', 'model', 'vocab')), parts along dimension 0
There are 2 independent parts. A program takes and returns all parts, laid end to end along the dimension named above; an argument that names none is the same for every part.
All inputs are finite; a program needn't handle non-finite values.
Results may differ from a plain program's by a relative error of at most 0.001.
Values are sent between devices in bfloat16 or wider.
A program may use at most 1 GiB of HBM per device.

v0:
```python
import jax
import jax.numpy as jnp
from jax import lax
from jax.sharding import PartitionSpec as P

value_a11 = 0.5
OWNER_SHARE = 4


def masked_softmax(scores, is_valid, target_pos):
    scores = jnp.where(is_valid, scores, -jnp.inf)
    top_score = jnp.max(scores, axis=1, keepdims=True)
    log_norm = top_score[:, 0] + jnp.log(jnp.sum(jnp.exp(scores - top_score), axis=1))
    probs = jnp.where(is_valid, jnp.exp(scores - log_norm[:, None]), 0.0)
    picked_score = jnp.take_along_axis(scores, target_pos[:, None], axis=1)[:, 0]
    return probs, picked_score - log_norm


def solution(mesh):
    shard_axes = ('model', 'vocab')
    num_shards = mesh.shape['model'] * mesh.shape['vocab']
    row_spec = P(('rep', 'model', 'vocab'), None)
    vec_spec = P(('rep', 'model', 'vocab'))

    def local_step(hidden, head_rows, allowed_ids, valid_mask, target_pos):
        rows_loc, list_len = allowed_ids.shape
        shard_len = head_rows.shape[0]
        row_cap = list_len // OWNER_SHARE
        is_valid = valid_mask > 0
        shard_of = allowed_ids // shard_len
        offset = allowed_ids - shard_of * shard_len
        owner_shard = jnp.where(is_valid, shard_of, num_shards)
        own_hits = (owner_shard[:, :, None] == jnp.arange(num_shards, dtype=jnp.int32)).astype(jnp.int32)
        slot_rank = jnp.maximum(jnp.sum(jnp.cumsum(own_hits, axis=1) * own_hits, axis=2) - 1, 0)
        row_idx = jnp.arange(rows_loc, dtype=jnp.int32)[:, None]
        send_ids = jnp.zeros((num_shards, rows_loc, row_cap), jnp.int32)
        send_ids = send_ids.at[owner_shard, row_idx, slot_rank].set(offset, mode='drop')
        hidden_all = lax.all_gather(hidden, shard_axes)
        recv_ids = lax.all_to_all(send_ids, shard_axes, 0, 0)
        picked = head_rows[recv_ids]
        part_scores = jnp.einsum('sbcd,sbd->sbc', picked, hidden_all, preferred_element_type=jnp.float32)
        back_scores = lax.all_to_all(part_scores, shard_axes, 0, 0)
        safe_owner = jnp.minimum(owner_shard, num_shards - 1)
        scores = back_scores[safe_owner, row_idx, slot_rank] / value_a11
        return masked_softmax(scores, is_valid, target_pos)

    program = jax.shard_map(local_step, mesh=mesh, in_specs=(row_spec, P(shard_axes, None), row_spec, row_spec, vec_spec), out_specs=(row_spec, vec_spec), check_vma=False)
    return program
```

profile of v0, /device:TPU:0, one launch (start us, length us, event | category | flops | bytes accessed | tf_op | source)
XLA Modules:
  0.0 541.2 jit_solution(1934609062158000721)
XLA Ops:
  7.2 0.0 all-gather.3.cloned.1.call-start
  7.2 0.7 all-gather.3.cloned.1.call-update
  7.9 1.3 fusion.5
  9.2 0.1 reshape.79
  9.3 0.1 copy.15
  9.4 1.7 select_reduce_fusion
  11.1 0.1 copy.16
  11.2 0.7 multiply_reduce_fusion
  11.9 0.7 and_reduce_fusion
  12.7 0.1 reshape.77
  12.8 8.1 %scatter_custom_fusion = s32[8192]{0:T(1024)S(1)} fusion(s32[2048]{0:T(1024)S(1)} %reshape.77, s32[2048]{0:T(1024)S(1)} %reshape.79, s32[]{:T(128)} %constant.19.clone.1), kind=kCustom, calls=%fused_computation.25 | custom fusion | bytes 32772
  20.8 0.1 reshape.53
  21.0 0.7 reshape.98
  21.7 7.4 %all-to-all-start = ((s32[16,1,512]{2,1,0:T(1,128)}), s32[16,1,512]{2,1,0:T(1,128)S(1)}, u32[]{:S(2)}, u32[]{:S(2)}) async-start(s32[16,1,512]{2,1,0:T(1,128)} %reshape.98), calls=%async_computation | async-start | bytes 65536 | tf_op jit(solution)/shard_map/all_to_all | solution.py:39
  29.1 0.7 fusion.15
  29.8 0.6 fusion.10
  30.4 0.6 add_bitcast_fusion
  31.0 4.8 all-to-all-done
  35.8 0.5 broadcast.161
  36.3 0.7 reduce.4
  37.0 0.1 reshape.99
  37.1 0.1 copy.17
  37.3 0.1 reshape.57
  37.4 225.4 %gather_fusion = bf16[8192,3072]{1,0:T(8,128)(2,1)} fusion(bf16[8016,3072]{1,0:T(8,128)(2,1)} %param.6, s32[8192]{0:T(1024)S(1)} %broadcast_clamp_fusion), kind=kCustom, calls=%fused_computation | custom fusion | bytes 100696064 | tf_op jit(solution)/shard_map/gather | solution.py:40
  262.8 0.0 copy-start.2
  262.8 0.0 copy-start
  262.8 0.0 all-gather.3.cloned.1.call-done
  262.8 0.0 copy-start.3
  262.8 21.8 %fusion = f32[16,32,1,16]{3,2,1,0:T(1,128)S(1)} fusion(bf16[16,32,16,3072]{3,2,1,0:T(8,128)(2,1)} %bitcast.38, bf16[16,32,3072,1]{2,1,0,3:T(8,128)(2,1)} %bitcast.39), kind=kOutput, calls=%fused_computation.4 | convolution fusion | flops 50331648 | bytes 53510144 | tf_op jit(solution)/shard_map/sbcd,sbd->sbc/dot_general | solution.py:41
  284.7 0.1 copy.19
  284.8 0.7 reshape.100
  285.5 221.2 %all-to-all-start.1 = ((f32[16,1,512]{2,1,0:T(1,128)}), f32[16,1,512]{2,1,0:T(1,128)S(1)}, u32[]{:S(2)}, u32[]{:S(2)}) async-start(f32[16,1,512]{2,1,0:T(1,128)} %reshape.100), calls=%async_computation.1 | async-start | bytes 65536 | tf_op jit(solution)/shard_map/all_to_all | solution.py:42
  506.8 0.0 copy-done.2
  506.8 0.0 copy-done
  506.8 0.1 reshape.63
  506.9 6.3 %all-to-all-done.1 = f32[16,1,512]{2,1,0:T(1,128)S(1)} async-done(((f32[16,1,512]{2,1,0:T(1,128)}), f32[16,1,512]{2,1,0:T(1,128)S(1)}, u32[]{:S(2)}, u32[]{:S(2)}) %all-to-all-start.1) | async-done | bytes 32800 | tf_op jit(solution)/shard_map/all_to_all | solution.py:42
  513.2 0.5 broadcast.162
  513.7 0.7 reduce.5
  514.4 0.1 reshape.101
  514.5 17.5 %gather_fusion.1 = f32[2048]{0:T(1024)S(1)} fusion(f32[16,32,16]{1,2,0:T(8,128)S(1)} %bitcast.37, s32[2048]{0:T(1024)S(1)} %reshape.63), kind=kCustom, calls=%fused_computation.1 | custom fusion | bytes 40960 | tf_op jit(solution)/shard_map/gather | solution.py:44
  532.0 0.1 reshape.88
  532.1 0.0 copy-done.1
  532.1 0.1 fusion.16
  532.2 0.7 gather_fusion.2
  532.9 0.2 exponential_reduce_fusion
  533.1 0.0 copy-done.3
  533.1 0.5 fusion.14
  533.6 0.7 exponential_select_fusion
  (11 shorter events, 0.1 us)
Async XLA Ops:
  7.2 255.7 %all-gather.3.cloned.1.call-start = ((), (), s32[]{:S(2)}) async-start(), calls=%async_computation.2 | async-start | bytes 3342336 | tf_op jit(solution)/shard_map/all_gather | solution.py:38
  21.7 14.1 %all-to-all-start = ((s32[16,1,512]{2,1,0:T(1,128)}), s32[16,1,512]{2,1,0:T(1,128)S(1)}, u32[]{:S(2)}, u32[]{:S(2)}) async-start(s32[16,1,512]{2,1,0:T(1,128)} %reshape.98), calls=%async_computation | async-start | bytes 65536 | tf_op jit(solution)/shard_map/all_to_all | solution.py:39
  262.8 243.9 %copy-start.2 = (s32[32,2]{0,1:T(2,128)S(1)}, s32[32,2]{0,1:T(2,128)}, u32[]{:S(2)}) copy-start(s32[32,2]{0,1:T(2,128)} %add_bitcast_fusion) | copy-start | bytes 772
  262.8 244.0 %copy-start = (s32[32,64,1]{1,0,2:T(8,128)S(1)}, s32[32,64,1]{1,0,2:T(8,128)}, u32[]{:S(2)}) copy-start(s32[32,64,1]{1,0,2:T(8,128)} %fusion.10) | copy-start | bytes 24580
  262.8 269.2 %copy-start.1 = (pred[32,64]{1,0:T(8,128)(4,1)S(1)}, pred[32,64]{1,0:T(8,128)(4,1)}, u32[]{:S(2)}) copy-start(pred[32,64]{1,0:T(8,128)(4,1)} %get-tuple-element.8) | copy-start | bytes 6148
  262.8 270.3 %copy-start.3 = (s32[32]{0:T(128)S(1)}, s32[32]{0:T(128)}, u32[]{:S(2)}) copy-start(s32[32]{0:T(128)} %param.9) | copy-start | bytes 388
  285.5 227.7 %all-to-all-start.1 = ((f32[16,1,512]{2,1,0:T(1,128)}), f32[16,1,512]{2,1,0:T(1,128)S(1)}, u32[]{:S(2)}, u32[]{:S(2)}) async-start(f32[16,1,512]{2,1,0:T(1,128)} %reshape.100), calls=%async_computation.1 | async-start | bytes 65536 | tf_op jit(solution)/shard_map/all_to_all | solution.py:42
Sparse Core Ops, SparseCore 0:
  10.3 48.1 all-gather.2
where the time goes:
time: 551 us; the launch traced here: 541 us
  local copies, waits for them, and re-layouts  255 us (46%)
  starting transfers between devices  229 us (42%)
  matrix products  21.8 us (4%)
  between operations  14.2 us (3%)
  waiting for transfers between devices  11.8 us (2%)
  other arithmetic  9.38 us (2%)
    gather x1, local copies, waits for them, and re-layouts, local_step(): picked = head_rows[recv_ids]  225 us
    all_to_all x1, starting transfers between devices, local_step(): back_scores = lax.all_to_all(part_scores, shard_axes, 0, 0)  221 us
    dot_general x1, matrix products, local_step(): jnp.einsum('sbcd,sbd->sbc', picked, hidden_all, preferred_element_type=jn...  21.8 us
    gather x1, local copies, waits for them, and re-layouts, local_step(): scores = back_scores[safe_owner, row_idx, slot_rank] / value_a11  17.5 us
  transfers between devices with their start and end apart: 3, of which 2 were waited for; matrix products, arithmetic and copies ran while one was open for 45% of the time, Pallas kernels for 0%

commit v1 on v0

v1 whole, which is shorter than its diff:
```python
import functools

import jax
import jax.numpy as jnp
from jax import lax
from jax.experimental import pallas as pl
from jax.experimental.pallas import tpu as pltpu
from jax.sharding import PartitionSpec as P

TEMPERATURE = 0.5
MESH = pl.DeviceIdType.MESH
PAIR = 512
NPAIR = 4
LANES = 128
HALVES = 2


def head_kernel(h_hbm, w_hbm, ids_hbm, ids_ref, valid_ref, tgt_ref, p_ref, lp_ref,
                w, h, ids_all, lane, tile, picks, back, sbuf0, sbuf1,
                w_sem, own_sem, own_ids_sem, h_recv, ids_recv, send_sem, back_send, back_recv):
    m = lax.axis_index('model')
    v = lax.axis_index('vocab')
    c = lax.rem(v, 2)
    y = v // 2
    me = m * 4 + v
    loc, width = h_hbm.shape
    shard_len = w_hbm.shape[0]
    list_len = ids_hbm.shape[1]
    half_w = width // HALVES
    rows_half = 8 * loc
    zbase = (m // 2) * 2
    zp = m + 1 - 2 * lax.rem(m, 2)
    far_near = jnp.where(m < 2, 2, 1)
    far_far = jnp.where(m < 2, 3, 0)
    v_sib = v + 1 - 2 * c
    v_y = lax.rem(v + 2, 4)
    dev_y = {'vocab': v_y}
    dev_zp = {'model': zp}
    dev_sib = {'vocab': v_sib}
    dev_fn = {'model': far_near}
    dev_ff = {'model': far_far}

    def w_copy(i):
        n_rows = min(PAIR, shard_len - i * PAIR)
        return pltpu.make_async_copy(w_hbm.at[pl.ds(i * PAIR, n_rows)], w.at[pl.ds(i * PAIR, n_rows)], w_sem.at[i])

    n_w = pl.cdiv(shard_len, PAIR)

    def h_unit(blk, half):
        return h.at[pl.ds(pl.multiple_of(blk * loc, loc), loc), pl.ds(half * half_w, half_w)]

    def ids_unit(blk):
        return ids_all.at[pl.ds(pl.multiple_of(blk * loc, loc), loc)]

    own_h = pltpu.make_async_copy(h_hbm, h.at[pl.ds(pl.multiple_of(me * loc, loc), loc)], own_sem)
    own_h.start()
    own_ids = pltpu.make_async_copy(ids_hbm, ids_unit(me), own_ids_sem)
    own_ids.start()
    for i in range(n_w):
        w_copy(i).start()

    barrier = pltpu.get_barrier_semaphore()
    peers = (dev_y, dev_zp, dev_sib, dev_fn, dev_ff)
    for d in peers:
        pl.semaphore_signal(barrier, inc=1, device_id=d, device_id_type=MESH)

    pending = []

    def h_copy(k, blk, half, dev):
        return pltpu.make_async_remote_copy(h_unit(blk, half), h_unit(blk, half), send_sem.at[k], h_recv.at[blk, half],
                                            device_id=dev, device_id_type=MESH)

    def ids_copy(k, blk, dev):
        return pltpu.make_async_remote_copy(ids_unit(blk), ids_unit(blk), send_sem.at[k], ids_recv.at[blk],
                                            device_id=dev, device_id_type=MESH)

    def send_h(blk, half, dev):
        h_copy(len(pending), blk, half, dev).start()
        pending.append(functools.partial(h_copy, len(pending), blk, half, dev))

    def send_ids(blk, dev):
        ids_copy(len(pending), blk, dev).start()
        pending.append(functools.partial(ids_copy, len(pending), blk, dev))

    def wait_h(blk, half):
        pltpu.make_async_remote_copy(h_unit(blk, half), h_unit(blk, half), send_sem.at[0], h_recv.at[blk, half],
                                     device_id=dev_sib, device_id_type=MESH).wait_recv()

    def wait_ids(blk):
        pltpu.make_async_remote_copy(ids_unit(blk), ids_unit(blk), send_sem.at[0], ids_recv.at[blk],
                                     device_id=dev_sib, device_id_type=MESH).wait_recv()

    def blk(zz, vv):
        return zz * 4 + vv

    b_y, b_z, b_d = blk(m, v_y), blk(zp, v), blk(zp, v_y)
    s_own, s_y, s_z, s_d = blk(m, v_sib), blk(m, lax.rem(v_sib + 2, 4)), blk(zp, v_sib), blk(zp, lax.rem(v_sib + 2, 4))
    b_fn, b_ff, b_fny, b_ffy = blk(far_near, v), blk(far_far, v), blk(far_near, v_y), blk(far_far, v_y)
    s_fn, s_ff = blk(far_near, v_sib), blk(far_far, v_sib)
    s_fny, s_ffy = blk(far_near, lax.rem(v_sib + 2, 4)), blk(far_far, lax.rem(v_sib + 2, 4))

    own_h.wait()
    own_ids.wait()
    pl.semaphore_wait(barrier, len(peers))

    send_h(me, 0, dev_y)
    send_h(me, 1, dev_zp)
    send_h(me, 1, dev_y)
    send_h(me, 0, dev_zp)
    send_h(me, 0, dev_sib)
    send_h(me, 1, dev_sib)
    for d in (dev_y, dev_zp, dev_sib):
        send_ids(me, d)

    wait_h(b_y, 0)
    send_h(b_y, 0, dev_zp)
    wait_h(b_z, 1)
    send_h(b_z, 1, dev_y)
    for d in (dev_fn, dev_ff):
        send_h(me, 0, d)
        send_h(me, 1, d)
        send_ids(me, d)
    send_h(b_y, 0, dev_sib)
    send_h(b_z, 1, dev_sib)
    wait_ids(b_y)
    send_ids(b_y, dev_zp)
    send_ids(b_y, dev_sib)
    wait_ids(b_z)
    send_ids(b_z, dev_sib)
    wait_h(b_y, 1)
    send_h(b_y, 1, dev_sib)
    wait_h(b_z, 0)
    send_h(b_z, 0, dev_sib)
    wait_ids(b_d)
    send_ids(b_d, dev_sib)
    for half in range(HALVES):
        wait_h(b_d, half)
        send_h(b_d, half, dev_sib)

    def far_first(b, half):
        wait_h(b, half)
        send_h(b, half, dev_y)
        send_h(b, half, dev_sib)

    def far_ids(b):
        wait_ids(b)
        send_ids(b, dev_y)
        send_ids(b, dev_sib)

    def far_second(b, half):
        wait_h(b, half)
        send_h(b, half, dev_sib)

    def point_0():
        pass

    def point_1():
        far_ids(b_fn)
        far_first(b_fn, 0)
        far_first(b_fn, 1)

    def point_2():
        wait_ids(b_fny)
        send_ids(b_fny, dev_sib)
        far_second(b_fny, 0)
        far_second(b_fny, 1)
        far_ids(b_ff)
        far_first(b_ff, 0)

    def point_3():
        far_first(b_ff, 1)

    def final_far():
        wait_ids(b_ffy)
        send_ids(b_ffy, dev_sib)
        far_second(b_ffy, 0)
        far_second(b_ffy, 1)
        for b in (s_fn, s_fny, s_ff, s_ffy):
            wait_ids(b)
            wait_h(b, 0)
            wait_h(b, 1)

    picks[...] = jnp.zeros_like(picks)

    def set_lists(r0):
        off = ids_all[pl.ds(r0, rows_half), :] - me * shard_len
        off = jnp.concatenate([off, off], axis=1)
        lane[...] = jnp.bitwise_and(off, LANES - 1)
        good = jnp.logical_and(off >= 0, off < shard_len)
        tile[...] = jnp.where(good, lax.shift_right_arithmetic(off, 7), 1 << 20)

    sbufs = (sbuf0, sbuf1)
    n_steps = w.shape[0] // (PAIR * NPAIR)

    def run_phase(r0, points):
        hr = pl.ds(r0, rows_half)

        def pick(s_ref, t0):
            for q in range(PAIR // LANES):
                g = jnp.take_along_axis(s_ref[:, q * LANES:(q + 1) * LANES], lane[...], axis=1)
                picks[hr, :] = jnp.where(tile[...] == t0 + q, g, picks[hr, :])

        def step(n, carry):
            for k, point in enumerate(points):
                if point is not None:
                    pl.when(n == k)(point)
            for j in range(NPAIR):
                rows = pl.ds(pl.multiple_of((n * NPAIR + j) * PAIR, PAIR), PAIR)
                sbufs[j % 2][...] = lax.dot_general(h[hr, :], w[rows, :], (((1,), (1,)), ((), ())),
                                                    preferred_element_type=jnp.float32)
                pick(sbufs[(j + 1) % 2], (n * NPAIR + j - 1) * (PAIR // LANES))
            return carry

        lax.fori_loop(0, n_steps, step, 0)
        pick(sbufs[(NPAIR - 1) % 2], (n_steps * NPAIR - 1) * (PAIR // LANES))

    def with_w(k, point):
        def run():
            for i in range(k * NPAIR, min((k + 1) * NPAIR, n_w)):
                w_copy(i).wait()
            point()
        return run

    def send_back(zz, vv, i):
        b = blk(zz, vv)
        cp = pltpu.make_async_remote_copy(picks.at[pl.ds(pl.multiple_of(b * loc, loc), loc)], back.at[me], back_send.at[i],
                                          back_recv.at[me], device_id={'model': zz, 'vocab': vv}, device_id_type=MESH)
        cp.start()
        return cp

    for b in (s_own, s_y, s_z, s_d):
        wait_ids(b)
        wait_h(b, 0)
        wait_h(b, 1)
    r_a = pl.multiple_of((m // 2) * rows_half, rows_half)
    r_b = pl.multiple_of((1 - m // 2) * rows_half, rows_half)
    set_lists(r_a)
    run_phase(r_a, [with_w(k, p) for k, p in enumerate((point_0, point_1, point_2, point_3))])
    backs = []
    for i, (zz, dv) in enumerate([(m, 1), (m, 2), (m, 3), (zp, 0), (zp, 1), (zp, 2), (zp, 3)]):
        backs.append(send_back(zz, lax.rem(v + dv, 4), i))
    final_far()
    set_lists(r_b)
    run_phase(r_b, [])
    for i, (zz, dv) in enumerate([(far_ff, dv) for far_ff in (far_far, far_near) for dv in range(4)]):
        backs.append(send_back(zz, lax.rem(v + dv, 4), 7 + i))

    back[me] = picks[pl.ds(pl.multiple_of(me * loc, loc), loc), :]
    total = back[me]
    for dz in range(4):
        for dv in range(4):
            if dz == 0 and dv == 0:
                continue
            b = blk(lax.rem(m + dz, 4), lax.rem(v + dv, 4))
            pltpu.make_async_remote_copy(back.at[b], back.at[b], back_send.at[0], back_recv.at[b],
                                         device_id=dev_sib, device_id_type=MESH).wait_recv()
            total = total + back[b]
    is_valid = valid_ref[...] > 0
    scores = jnp.where(is_valid, total[:, :list_len] / TEMPERATURE, -jnp.inf)
    top = jnp.max(scores, axis=1, keepdims=True)
    log_norm = top + jnp.log(jnp.sum(jnp.exp(scores - top), axis=1, keepdims=True))
    p_ref[...] = jnp.where(is_valid, jnp.exp(scores - log_norm), 0.0)
    eye = lax.broadcasted_iota(jnp.int32, (loc, loc), 0) == lax.broadcasted_iota(jnp.int32, (loc, loc), 1)
    tgt_col = jnp.sum(jnp.where(eye, tgt_ref[...], 0), axis=1, keepdims=True)
    hit = lax.broadcasted_iota(jnp.int32, (loc, list_len), 1) == tgt_col
    picked = jnp.sum(jnp.where(hit, scores, 0.0), axis=1, keepdims=True)
    lp_ref[...] = jnp.sum(jnp.where(eye, picked - log_norm, 0.0), axis=0, keepdims=True)
    for make in pending:
        make().wait_send()
    for cp in backs:
        cp.wait_send()


def solution(mesh):
    axes = ('model', 'vocab')
    row_spec = P(('rep',) + axes, None)
    vec_spec = P(('rep',) + axes)

    def local_step(hidden, head_rows, allowed_ids, valid_mask, target_pos):
        loc, width = hidden.shape
        list_len = allowed_ids.shape[1]
        rows = 16 * loc
        block = PAIR * NPAIR
        w_rows = pl.cdiv(head_rows.shape[0], block) * block
        any_spec = pl.BlockSpec(memory_space=pl.ANY)
        vmem = pl.BlockSpec(memory_space=pltpu.VMEM)
        dma = pltpu.SemaphoreType.DMA
        p, lp = pl.pallas_call(
            head_kernel,
            out_shape=(jax.ShapeDtypeStruct((loc, list_len), jnp.float32), jax.ShapeDtypeStruct((1, loc), jnp.float32)),
            in_specs=[any_spec, any_spec, any_spec, vmem, vmem, vmem],
            out_specs=(vmem, vmem),
            scratch_shapes=[
                pltpu.VMEM((w_rows, width), jnp.bfloat16),
                pltpu.VMEM((rows, width), jnp.bfloat16),
                pltpu.VMEM((rows, list_len), jnp.int32),
                pltpu.VMEM((rows // 2, LANES), jnp.int32),
                pltpu.VMEM((rows // 2, LANES), jnp.int32),
                pltpu.VMEM((rows, LANES), jnp.float32),
                pltpu.VMEM((16, loc, LANES), jnp.float32),
                pltpu.VMEM((rows // 2, PAIR), jnp.float32),
                pltpu.VMEM((rows // 2, PAIR), jnp.float32),
                dma((pl.cdiv(head_rows.shape[0], PAIR),)),
                dma, dma,
                dma((16, HALVES)),
                dma((16,)),
                dma((64,)),
                dma((16,)),
                dma((16,)),
            ],
            compiler_params=pltpu.CompilerParams(collective_id=0, has_side_effects=True, vmem_limit_bytes=67043328),
        )(hidden, head_rows, allowed_ids, allowed_ids, valid_mask, target_pos.reshape(1, loc))
        return p, lp.reshape(loc)

    return jax.shard_map(local_step, mesh=mesh, in_specs=(row_spec, P(axes, None), row_spec, row_spec, vec_spec),
                         out_specs=(row_spec, vec_spec), check_vma=False)
```

time: 551 us -> 83.2 us (0.15); the launches traced: 541 us -> 82.8 us
  local copies, waits for them, and re-layouts: 255 us -> 2.46 us
  starting transfers between devices: 229 us -> 0 us
  Pallas kernels: 0 us -> 79.7 us
  matrix products: 21.8 us -> 0 us
  between operations: 14.2 us -> 0.64 us
  waiting for transfers between devices: 11.8 us -> 0 us
  other arithmetic: 9.38 us -> 0 us
    gather x3 -> x0, local copies, waits for them, and re-layouts: 244 us -> none  [the longest x1 225 us: local_step(): picked = head_rows[recv_ids]]
    all_to_all x2 -> x0, starting transfers between devices: 229 us -> none  [the longest x1 221 us: local_step(): back_scores = lax.all_to_all(part_scores, shard_axes, 0, 0)]
    pallas_call x0 -> x1, Pallas kernels: none -> 79.7 us  [local_step(): pl.pallas_call(head_kernel, out_shape=(jax.ShapeDtypeStruct((loc, list_le...]
    dot_general x1 -> x0, matrix products: 21.8 us -> none  [local_step(): jnp.einsum('sbcd,sbd->sbc', picked, hidden_all, preferred_element_type=jn...]
    all_to_all x2 -> x0, waiting for transfers between devices: 11.1 us -> none  [the longest x1 6.32 us: local_step(): back_scores = lax.all_to_all(part_scores, shard_axes, 0, 0)]
    unnamed x18 -> x2, local copies, waits for them, and re-layouts: 9.9 us -> 2.46 us
  transfers between devices with their start and end apart: 3 -> 0, of which waited for: 2 -> 0; matrix products, arithmetic and copies ran while one was open for 45% -> 0% of each run, Pallas kernels for 0% -> 0%
where the time goes in v1:
time: 83.2 us; the launch traced here: 82.8 us
  Pallas kernels  79.7 us (96%)
  local copies, waits for them, and re-layouts  2.46 us (3%)
    pallas_call x1, Pallas kernels, local_step(): pl.pallas_call(head_kernel, out_shape=(jax.ShapeDtypeStruct((loc, list_le...  79.7 us
    unnamed x2, local copies, waits for them, and re-layouts  2.46 us

profile of v1, /device:TPU:0, one launch (start us, length us, event | category | flops | bytes accessed | tf_op | source)
XLA Modules:
  0.0 82.8 jit_solution(10849911636079279632)
XLA Ops:
  0.6 79.7 %shard_map.68 = (f32[32,64]{1,0:T(8,128)}, f32[1,32]{1,0:T(1,128)}) custom-call(bf16[32,3072]{1,0:T(8,128)(2,1)} %h_hbm.1, bf16[8016,3072]{1,0:T(8,128)(2,1)} %w_hbm.1, s32[32,64]{1,0:T(8,128)} %ids_ref.1, s32[32,64]{1,0:T(8,128)} %ids_ref.1, s32[32,64]{1,0:T(8,128)} %valid_ref.1, s32[1,32]{1,0:T(1,128)} %bitcast.2), custom_call_target="tpu_custom_call" | custom-call | tf_op jit(solution)/shard_map/pallas_call | solution.py:288
  80.4 1.3 %copy.9 = f32[32,64]{1,0:T(8,128)} copy(f32[32,64]{1,0:T(8,128)} %get-tuple-element.8) | data formatting | bytes 16384
  81.7 1.1 %copy.10 = f32[32]{0:T(128)} copy(f32[32]{0:T(128)} %bitcast.3) | data formatting | bytes 256

commit v2 on v1

v2 whole, which is shorter than its diff:
```python
import functools

import jax
import jax.numpy as jnp
from jax import lax
from jax.experimental import pallas as pl
from jax.experimental.pallas import tpu as pltpu
from jax.sharding import PartitionSpec as P

TEMPERATURE = 0.5
MESH = pl.DeviceIdType.MESH
PAIR = 512
NPAIR = 4
LANES = 128
W_ROWS = 1024
CHUNKS_PER_STEP = PAIR * NPAIR // W_ROWS
ALL, INNER, OUTER = 0, 1, 2


def head_kernel(h_hbm, w_hbm, ids_hbm, valid_ref, tgt_ref, p_ref, lp_ref,
                w, h, acc, ids_all, lane, tile, picks, packed, back, sbuf0, sbuf1,
                w_sem, own_sem, own_ids_sem, h_recv, ids_recv, send_sem, back_send, back_recv):
    m = lax.axis_index('model')
    v = lax.axis_index('vocab')
    c = lax.rem(v, 2)
    me = m * 4 + v
    loc, width = h_hbm.shape
    shard_len = w_hbm.shape[0]
    list_len = ids_hbm.shape[1]
    quarter = width // 4
    half_w = width // 2
    rows_half = 8 * loc
    zp = m + 1 - 2 * lax.rem(m, 2)
    inner_n = m * (3 - m) // 2
    inner = inner_n == 1
    far_near = jnp.where(m < 2, 2, 1)
    far_far = jnp.where(m < 2, 3, 0)
    v_sib = v + 1 - 2 * c
    v_y = lax.rem(v + 2, 4)
    v_sy = lax.rem(v_sib + 2, 4)
    dev_y = {'vocab': v_y}
    dev_zp = {'model': zp}
    dev_sib = {'vocab': v_sib}
    dev_across = {'model': jnp.where(m < 2, 2, 1)}
    near_peers = (dev_y, dev_zp, dev_sib)

    n_chunks = pl.cdiv(shard_len, W_ROWS)

    def w_copy(i, half):
        n_rows = min(W_ROWS, shard_len - i * W_ROWS)
        at = (pl.ds(i * W_ROWS, n_rows), pl.ds(half * half_w, half_w))
        return pltpu.make_async_copy(w_hbm.at[at], w.at[at], w_sem.at[i, half])

    def row_block(blk):
        return pl.ds(pl.multiple_of(blk * loc, loc), loc)

    own_h = pltpu.make_async_copy(h_hbm, h.at[row_block(me)], own_sem)
    own_h.start()
    own_ids = pltpu.make_async_copy(ids_hbm, ids_all.at[row_block(me)], own_ids_sem)
    own_ids.start()
    barrier = pltpu.get_barrier_semaphore()
    for d in near_peers:
        pl.semaphore_signal(barrier, inc=1, device_id=d, device_id_type=MESH)

    @pl.when(inner)
    def _():
        pl.semaphore_signal(barrier, inc=1, device_id=dev_across, device_id_type=MESH)

    for half in range(2):
        for i in range(n_chunks):
            w_copy(i, half).start(priority=1)

    sent = {ALL: [], INNER: []}
    n_sent = [0]

    def h_copy(k, blk, piece, dev):
        ref = h.at[row_block(blk), pl.ds(piece[0] * quarter, piece[1] * quarter)]
        return pltpu.make_async_remote_copy(ref, ref, send_sem.at[k], h_recv.at[blk, piece[0]],
                                            device_id=dev, device_id_type=MESH)

    def ids_copy(k, blk, dev):
        ref = ids_all.at[row_block(blk)]
        return pltpu.make_async_remote_copy(ref, ref, send_sem.at[k], ids_recv.at[blk],
                                            device_id=dev, device_id_type=MESH)

    def start(make, who):
        make(n_sent[0]).start()
        sent[who].append(functools.partial(make, n_sent[0]))
        n_sent[0] += 1

    def send_h(blk, piece, dev, who=0):
        start(lambda k: h_copy(k, blk, piece, dev), who)

    def send_ids(blk, dev, who=0):
        start(lambda k: ids_copy(k, blk, dev), who)

    def wait_h(blk, piece):
        h_copy(0, blk, piece, dev_sib).wait_recv()

    def wait_ids(blk):
        ids_copy(0, blk, dev_sib).wait_recv()

    def blk(zz, vv):
        return zz * 4 + vv

    b_y, b_z, b_d = blk(m, v_y), blk(zp, v), blk(zp, v_y)
    near_sib = (blk(m, v_sib), blk(m, v_sy), blk(zp, v_sib), blk(zp, v_sy))
    b_fn, b_ff, b_fny, b_ffy = blk(far_near, v), blk(far_far, v), blk(far_near, v_y), blk(far_far, v_y)
    far_sib = (blk(far_near, v_sib), blk(far_far, v_sib), blk(far_near, v_sy), blk(far_far, v_sy))
    quarters = tuple((q, 1) for q in range(4))
    halves = ((0, 2), (2, 2))

    own_h.wait()
    own_ids.wait()
    pl.semaphore_wait(barrier, 3 + inner_n)

    send_h(me, quarters[0], dev_y)
    send_h(me, quarters[1], dev_zp)
    send_h(me, quarters[1], dev_y)
    send_h(me, quarters[0], dev_zp)

    @pl.when(inner)
    def _():
        send_h(me, halves[0], dev_across, INNER)

    send_h(me, halves[0], dev_sib)
    wait_h(b_y, quarters[0])
    send_h(b_y, quarters[0], dev_zp)
    wait_h(b_z, quarters[1])
    send_h(b_z, quarters[1], dev_y)
    send_h(me, quarters[2], dev_y)
    send_h(me, quarters[3], dev_zp)
    send_h(me, quarters[3], dev_y)
    send_h(me, quarters[2], dev_zp)
    send_h(me, halves[1], dev_sib)
    for d in near_peers:
        send_ids(me, d)
    wait_h(b_y, quarters[1])
    send_h(b_y, halves[0], dev_sib)
    wait_h(b_z, quarters[0])
    send_h(b_z, halves[0], dev_sib)

    @pl.when(inner)
    def _():
        send_h(b_z, halves[0], dev_across, INNER)
        send_h(me, halves[1], dev_across, INNER)
        send_ids(me, dev_across, INNER)

    def far(b, half):
        wait_h(b, halves[half])
        send_h(b, halves[half], dev_y, INNER)
        send_h(b, halves[half], dev_zp, INNER)
        send_h(b, halves[half], dev_sib, INNER)
        if half:
            wait_ids(b)
            for d in (dev_y, dev_zp, dev_sib):
                send_ids(b, d, INNER)

    def far_outer(b, half):
        wait_h(b, halves[half])
        send_h(b, halves[half], dev_y, OUTER)
        send_h(b, halves[half], dev_sib, OUTER)
        if half:
            wait_ids(b)
            for d in (dev_y, dev_sib):
                send_ids(b, d, OUTER)

    def far_y(b, half, who):
        wait_h(b, halves[half])
        send_h(b, halves[half], dev_sib, who)
        if half:
            wait_ids(b)
            send_ids(b, dev_sib, who)

    sent[OUTER] = []
    outer = inner_n == 0

    pl.when(inner)(lambda: far(b_fn, 0))
    wait_h(b_d, quarters[0])
    wait_h(b_d, quarters[1])
    send_h(b_d, halves[0], dev_sib)
    for b in near_sib:
        wait_h(b, halves[0])

    def wait_w(i, half):
        for k in range(CHUNKS_PER_STEP):
            if i * CHUNKS_PER_STEP + k < n_chunks:
                w_copy(i * CHUNKS_PER_STEP + k, half).wait()

    def a0_0():
        wait_w(0, 0)

    def a0_1():
        wait_w(1, 0)
        wait_h(b_y, quarters[2])
        send_h(b_y, quarters[2], dev_zp)
        wait_h(b_z, quarters[3])
        send_h(b_z, quarters[3], dev_y)
        wait_h(b_y, quarters[3])
        send_h(b_y, halves[1], dev_sib)
        wait_h(b_z, quarters[2])
        send_h(b_z, halves[1], dev_sib)
        wait_ids(b_y)
        send_ids(b_y, dev_zp)
        send_ids(b_y, dev_sib)
        wait_ids(b_z)
        send_ids(b_z, dev_sib)

        @pl.when(inner)
        def _():
            send_h(b_z, halves[1], dev_across, INNER)
            send_ids(b_z, dev_across, INNER)
            far(b_ff, 0)

    def a0_2():
        wait_w(2, 0)

        @pl.when(inner)
        def _():
            far(b_fn, 1)
            far_y(b_fny, 0, INNER)

        pl.when(outer)(lambda: far_outer(b_fn, 0))

    def a0_3():
        wait_w(3, 0)
        wait_h(b_d, quarters[2])
        wait_h(b_d, quarters[3])
        send_h(b_d, halves[1], dev_sib)
        wait_ids(b_d)
        send_ids(b_d, dev_sib)

    def a1_0():
        wait_w(0, 1)

        @pl.when(inner)
        def _():
            far(b_ff, 1)
            far_y(b_ffy, 0, INNER)

        pl.when(outer)(lambda: far_outer(b_ff, 0))

    def a1_1():
        wait_w(1, 1)
        pl.when(outer)(lambda: far_y(b_fny, 0, OUTER))

    def a1_2():
        wait_w(2, 1)
        pl.when(inner)(lambda: far_y(b_fny, 1, INNER))
        pl.when(outer)(lambda: far_outer(b_fn, 1))

    def a1_3():
        wait_w(3, 1)
        pl.when(inner)(lambda: far_y(b_ffy, 1, INNER))

        @pl.when(outer)
        def _():
            far_outer(b_ff, 1)
            far_y(b_ffy, 0, OUTER)

    def b0_1():
        pl.when(outer)(lambda: far_y(b_fny, 1, OUTER))

    def b0_2():
        pl.when(outer)(lambda: far_y(b_ffy, 1, OUTER))

    picks[...] = jnp.zeros_like(picks)

    def set_lists(r0):
        off = ids_all[pl.ds(r0, rows_half), :] - me * shard_len
        off = jnp.concatenate([off, off], axis=1)
        lane[...] = jnp.bitwise_and(off, LANES - 1)
        good = jnp.logical_and(off >= 0, off < shard_len)
        tile[...] = jnp.where(good, lax.shift_right_arithmetic(off, 7), 1 << 20)

    sbufs = (sbuf0, sbuf1)
    n_steps = w.shape[0] // (PAIR * NPAIR)

    def run_phase(r0, half, points):
        hr = pl.ds(r0, rows_half)
        kc = pl.ds(half * half_w, half_w)

        def pick(s_ref, t0):
            for q in range(PAIR // LANES):
                g = jnp.take_along_axis(s_ref[:, q * LANES:(q + 1) * LANES], lane[...], axis=1)
                picks[hr, :] = jnp.where(tile[...] == t0 + q, g, picks[hr, :])

        def step(n, carry):
            for k, point in enumerate(points):
                if point is not None:
                    pl.when(n == k)(point)
            for j in range(NPAIR):
                rows = pl.ds(pl.multiple_of((n * NPAIR + j) * PAIR, PAIR), PAIR)
                prod = lax.dot_general(h[hr, kc], w[rows, kc], (((1,), (1,)), ((), ())),
                                       preferred_element_type=jnp.float32)
                if half == 0:
                    acc[n * NPAIR + j] = prod
                else:
                    sbufs[j % 2][...] = prod + acc[n * NPAIR + j]
                    pick(sbufs[(j + 1) % 2], (n * NPAIR + j - 1) * (PAIR // LANES))
            return carry

        lax.fori_loop(0, n_steps, step, 0)
        if half:
            pick(sbufs[(NPAIR - 1) % 2], (n_steps * NPAIR - 1) * (PAIR // LANES))

    low = lax.broadcasted_iota(jnp.int32, (loc // 2, LANES), 1) < list_len

    def pack(r0, p0):
        for i in range(8):
            top = picks[pl.ds(pl.multiple_of(r0 + i * loc, loc // 2), loc // 2), :]
            bot = picks[pl.ds(pl.multiple_of(r0 + i * loc + loc // 2, loc // 2), loc // 2), :]
            packed[p0 + i] = jnp.where(low, top, bot)

    def send_back(zz, vv, i):
        cp = pltpu.make_async_remote_copy(packed.at[blk(zz, vv)], back.at[me], back_send.at[i], back_recv.at[me],
                                          device_id={'model': zz, 'vocab': vv}, device_id_type=MESH)
        cp.start()
        return cp

    r_a = pl.multiple_of((m // 2) * rows_half, rows_half)
    r_b = pl.multiple_of((1 - m // 2) * rows_half, rows_half)
    run_phase(r_a, 0, (a0_0, a0_1, a0_2, a0_3))
    for b in near_sib:
        wait_ids(b)
        wait_h(b, halves[1])
    set_lists(r_a)
    run_phase(r_a, 1, (a1_0, a1_1, a1_2, a1_3))
    pack(r_a, (m // 2) * 8)
    backs = []
    for i, (zz, dv) in enumerate([(zp, 2), (zp, 3), (zp, 0), (zp, 1), (m, 2), (m, 1), (m, 3)]):
        backs.append(send_back(zz, lax.rem(v + dv, 4), i))
    for b in far_sib:
        wait_h(b, halves[0])
    run_phase(r_b, 0, (None, b0_1, b0_2))
    for b in far_sib:
        wait_ids(b)
        wait_h(b, halves[1])
    set_lists(r_b)
    run_phase(r_b, 1, ())
    pack(r_b, (1 - m // 2) * 8)
    for i, (zz, dv) in enumerate([(zf, dv) for zf in (far_far, far_near) for dv in (2, 3, 0, 1)]):
        backs.append(send_back(zz, lax.rem(v + dv, 4), 7 + i))

    back[me] = packed[me]
    total = back[me]
    for dz in range(4):
        for dv in range(4):
            if dz == 0 and dv == 0:
                continue
            b = blk(lax.rem(m + dz, 4), lax.rem(v + dv, 4))
            pltpu.make_async_remote_copy(back.at[b], back.at[b], back_send.at[0], back_recv.at[b],
                                         device_id=dev_sib, device_id_type=MESH).wait_recv()
            total = total + back[b]
    total = jnp.concatenate([total, pltpu.roll(total, LANES - list_len, 1)], axis=0)[:, :list_len]
    is_valid = valid_ref[...] > 0
    scores = jnp.where(is_valid, total / TEMPERATURE, -jnp.inf)
    top = jnp.max(scores, axis=1, keepdims=True)
    log_norm = top + jnp.log(jnp.sum(jnp.exp(scores - top), axis=1, keepdims=True))
    p_ref[...] = jnp.where(is_valid, jnp.exp(scores - log_norm), 0.0)
    eye = lax.broadcasted_iota(jnp.int32, (loc, loc), 0) == lax.broadcasted_iota(jnp.int32, (loc, loc), 1)
    tgt_col = jnp.sum(jnp.where(eye, tgt_ref[...], 0), axis=1, keepdims=True)
    hit = lax.broadcasted_iota(jnp.int32, (loc, list_len), 1) == tgt_col
    picked = jnp.sum(jnp.where(hit, scores, 0.0), axis=1, keepdims=True)
    lp_ref[...] = jnp.sum(jnp.where(eye, picked - log_norm, 0.0), axis=0, keepdims=True)
    for make in sent[ALL]:
        make().wait_send()

    @pl.when(inner)
    def _():
        for make in sent[INNER]:
            make().wait_send()

    @pl.when(outer)
    def _():
        for make in sent[OUTER]:
            make().wait_send()

    for cp in backs:
        cp.wait_send()


def solution(mesh):
    axes = ('model', 'vocab')
    row_spec = P(('rep',) + axes, None)
    vec_spec = P(('rep',) + axes)

    def local_step(hidden, head_rows, allowed_ids, valid_mask, target_pos):
        loc, width = hidden.shape
        list_len = allowed_ids.shape[1]
        rows = 16 * loc
        block = PAIR * NPAIR
        w_rows = pl.cdiv(head_rows.shape[0], block) * block
        any_spec = pl.BlockSpec(memory_space=pl.ANY)
        vmem = pl.BlockSpec(memory_space=pltpu.VMEM)
        dma = pltpu.SemaphoreType.DMA
        p, lp = pl.pallas_call(
            head_kernel,
            out_shape=(jax.ShapeDtypeStruct((loc, list_len), jnp.float32), jax.ShapeDtypeStruct((1, loc), jnp.float32)),
            in_specs=[any_spec, any_spec, any_spec, vmem, vmem],
            out_specs=(vmem, vmem),
            scratch_shapes=[
                pltpu.VMEM((w_rows, width), jnp.bfloat16),
                pltpu.VMEM((rows, width), jnp.bfloat16),
                pltpu.VMEM((w_rows // PAIR, rows // 2, PAIR), jnp.float32),
                pltpu.VMEM((rows, list_len), jnp.int32),
                pltpu.VMEM((rows // 2, LANES), jnp.int32),
                pltpu.VMEM((rows // 2, LANES), jnp.int32),
                pltpu.VMEM((rows, LANES), jnp.float32),
                pltpu.VMEM((16, loc // 2, LANES), jnp.float32),
                pltpu.VMEM((16, loc // 2, LANES), jnp.float32),
                pltpu.VMEM((rows // 2, PAIR), jnp.float32),
                pltpu.VMEM((rows // 2, PAIR), jnp.float32),
                dma((pl.cdiv(head_rows.shape[0], W_ROWS), 2)),
                dma, dma,
                dma((16, 4)),
                dma((16,)),
                dma((96,)),
                dma((16,)),
                dma((16,)),
            ],
            compiler_params=pltpu.CompilerParams(collective_id=0, has_side_effects=True, vmem_limit_bytes=67043328),
        )(hidden, head_rows, allowed_ids, valid_mask, target_pos.reshape(1, loc))
        return p, lp.reshape(loc)

    return jax.shard_map(local_step, mesh=mesh, in_specs=(row_spec, P(axes, None), row_spec, row_spec, vec_spec),
                         out_specs=(row_spec, vec_spec), check_vma=False)
```

time: 83.2 us -> 55.7 us (0.67)
  Pallas kernels: 79.7 us -> 52.3 us
    pallas_call x1, Pallas kernels: 79.7 us -> 52.3 us  [local_step(): pl.pallas_call(head_kernel, out_shape=(jax.ShapeDtypeStruct((loc, list_le...]
where the time goes in v2:
time: 55.7 us; the launch traced here: 55.4 us
  Pallas kernels  52.3 us (94%)
  local copies, waits for them, and re-layouts  2.46 us (4%)
  between operations  0.64 us (1%)
    pallas_call x1, Pallas kernels, local_step(): pl.pallas_call(head_kernel, out_shape=(jax.ShapeDtypeStruct((loc, list_le...  52.3 us
    unnamed x2, local copies, waits for them, and re-layouts  2.46 us

profile of v2, /device:TPU:0, one launch (start us, length us, event | category | flops | bytes accessed | tf_op | source)
XLA Modules:
  0.0 55.4 jit_solution(15009620049237949490)
XLA Ops:
  0.6 52.3 %shard_map.68 = (f32[32,64]{1,0:T(8,128)}, f32[1,32]{1,0:T(1,128)}) custom-call(bf16[32,3072]{1,0:T(8,128)(2,1)} %h_hbm.1, bf16[8016,3072]{1,0:T(8,128)(2,1)} %w_hbm.1, s32[32,64]{1,0:T(8,128)} %ids_hbm.1, s32[32,64]{1,0:T(8,128)} %valid_ref.1, s32[1,32]{1,0:T(1,128)} %bitcast.2), custom_call_target="tpu_custom_call" | custom-call | tf_op jit(solution)/shard_map/pallas_call | solution.py:397
  52.9 1.3 %copy.9 = f32[32,64]{1,0:T(8,128)} copy(f32[32,64]{1,0:T(8,128)} %get-tuple-element.8) | data formatting | bytes 16384
  54.2 1.1 %copy.10 = f32[32]{0:T(128)} copy(f32[32]{0:T(128)} %bitcast.3) | data formatting | bytes 256

commit v3 on v2

--- a/solution.py
+++ b/solution.py
@@ -10,16 +10,14 @@
 TEMPERATURE = 0.5
 MESH = pl.DeviceIdType.MESH
 PAIR = 512
-NPAIR = 4
 LANES = 128
 W_ROWS = 1024
-CHUNKS_PER_STEP = PAIR * NPAIR // W_ROWS
 ALL, INNER, OUTER = 0, 1, 2
 
 
-def head_kernel(h_hbm, w_hbm, ids_hbm, valid_ref, tgt_ref, p_ref, lp_ref,
-                w, h, acc, ids_all, lane, tile, picks, packed, back, sbuf0, sbuf1,
-                w_sem, own_sem, own_ids_sem, h_recv, ids_recv, send_sem, back_send, back_recv):
+def head_kernel(h_hbm, w_hbm, ids_hbm, valid_hbm, tgt_hbm, p_ref, lp_ref,
+                valid_ref, tgt_ref, w, h, acc, ids_all, lane, tile, picks, packed, back, sbuf0, sbuf1,
+                w_sem, own_sem, own_ids_sem, valid_sem, tgt_sem, h_recv, ids_recv, send_sem, back_send, back_recv):
     m = lax.axis_index('model')
     v = lax.axis_index('vocab')
     c = lax.rem(v, 2)
@@ -54,10 +52,6 @@
     def row_block(blk):
         return pl.ds(pl.multiple_of(blk * loc, loc), loc)
 
-    own_h = pltpu.make_async_copy(h_hbm, h.at[row_block(me)], own_sem)
-    own_h.start()
-    own_ids = pltpu.make_async_copy(ids_hbm, ids_all.at[row_block(me)], own_ids_sem)
-    own_ids.start()
     barrier = pltpu.get_barrier_semaphore()
     for d in near_peers:
         pl.semaphore_signal(barrier, inc=1, device_id=d, device_id_type=MESH)
@@ -66,6 +60,14 @@
     def _():
         pl.semaphore_signal(barrier, inc=1, device_id=dev_across, device_id_type=MESH)
 
+    own_h = pltpu.make_async_copy(h_hbm, h.at[row_block(me)], own_sem)
+    own_h.start()
+    own_valid = pltpu.make_async_copy(valid_hbm, valid_ref, valid_sem)
+    own_tgt = pltpu.make_async_copy(tgt_hbm, tgt_ref, tgt_sem)
+    own_ids = pltpu.make_async_copy(ids_hbm, ids_all.at[row_block(me)], own_ids_sem)
+    own_ids.start()
+    own_valid.start()
+    own_tgt.start()
     for half in range(2):
         for i in range(n_chunks):
             w_copy(i, half).start(priority=1)
@@ -179,23 +181,18 @@
     wait_h(b_d, quarters[0])
     wait_h(b_d, quarters[1])
     send_h(b_d, halves[0], dev_sib)
+    wait_h(b_y, quarters[2])
+    send_h(b_y, quarters[2], dev_zp)
+    wait_h(b_z, quarters[3])
+    send_h(b_z, quarters[3], dev_y)
     for b in near_sib:
         wait_h(b, halves[0])
 
-    def wait_w(i, half):
-        for k in range(CHUNKS_PER_STEP):
-            if i * CHUNKS_PER_STEP + k < n_chunks:
-                w_copy(i * CHUNKS_PER_STEP + k, half).wait()
-
-    def a0_0():
-        wait_w(0, 0)
-
-    def a0_1():
-        wait_w(1, 0)
-        wait_h(b_y, quarters[2])
-        send_h(b_y, quarters[2], dev_zp)
-        wait_h(b_z, quarters[3])
-        send_h(b_z, quarters[3], dev_y)
+    def wait_w(half):
+        for i in range(n_chunks):
+            w_copy(i, half).wait()
+
+    def a0_quarter():
         wait_h(b_y, quarters[3])
         send_h(b_y, halves[1], dev_sib)
         wait_h(b_z, quarters[2])
@@ -212,9 +209,7 @@
             send_ids(b_z, dev_across, INNER)
             far(b_ff, 0)
 
-    def a0_2():
-        wait_w(2, 0)
-
+    def a0_half():
         @pl.when(inner)
         def _():
             far(b_fn, 1)
@@ -222,17 +217,14 @@
 
         pl.when(outer)(lambda: far_outer(b_fn, 0))
 
-    def a0_3():
-        wait_w(3, 0)
+    def a0_three():
         wait_h(b_d, quarters[2])
         wait_h(b_d, quarters[3])
         send_h(b_d, halves[1], dev_sib)
         wait_ids(b_d)
         send_ids(b_d, dev_sib)
 
-    def a1_0():
-        wait_w(0, 1)
-
+    def a1_start():
         @pl.when(inner)
         def _():
             far(b_ff, 1)
@@ -240,17 +232,15 @@
 
         pl.when(outer)(lambda: far_outer(b_ff, 0))
 
-    def a1_1():
-        wait_w(1, 1)
-        pl.when(outer)(lambda: far_y(b_fny, 0, OUTER))
-
-    def a1_2():
-        wait_w(2, 1)
+    def a1_quarter():
         pl.when(inner)(lambda: far_y(b_fny, 1, INNER))
-        pl.when(outer)(lambda: far_outer(b_fn, 1))
-
-    def a1_3():
-        wait_w(3, 1)
+
+        @pl.when(outer)
+        def _():
+            far_outer(b_fn, 1)
+            far_y(b_fny, 0, OUTER)
+
+    def a1_three():
         pl.when(inner)(lambda: far_y(b_ffy, 1, INNER))
 
         @pl.when(outer)
@@ -258,11 +248,11 @@
             far_outer(b_ff, 1)
             far_y(b_ffy, 0, OUTER)
 
-    def b0_1():
-        pl.when(outer)(lambda: far_y(b_fny, 1, OUTER))
-
-    def b0_2():
-        pl.when(outer)(lambda: far_y(b_ffy, 1, OUTER))
+    def b0_half():
+        @pl.when(outer)
+        def _():
+            far_y(b_fny, 1, OUTER)
+            far_y(b_ffy, 1, OUTER)
 
     picks[...] = jnp.zeros_like(picks)
 
@@ -274,9 +264,9 @@
         tile[...] = jnp.where(good, lax.shift_right_arithmetic(off, 7), 1 << 20)
 
     sbufs = (sbuf0, sbuf1)
-    n_steps = w.shape[0] // (PAIR * NPAIR)
-
-    def run_phase(r0, half, points):
+    n_pairs = w.shape[0] // PAIR
+
+    def run_pass(r0, half, points):
         hr = pl.ds(r0, rows_half)
         kc = pl.ds(half * half_w, half_w)
 
@@ -285,24 +275,19 @@
                 g = jnp.take_along_axis(s_ref[:, q * LANES:(q + 1) * LANES], lane[...], axis=1)
                 picks[hr, :] = jnp.where(tile[...] == t0 + q, g, picks[hr, :])
 
-        def step(n, carry):
-            for k, point in enumerate(points):
-                if point is not None:
-                    pl.when(n == k)(point)
-            for j in range(NPAIR):
-                rows = pl.ds(pl.multiple_of((n * NPAIR + j) * PAIR, PAIR), PAIR)
-                prod = lax.dot_general(h[hr, kc], w[rows, kc], (((1,), (1,)), ((), ())),
-                                       preferred_element_type=jnp.float32)
-                if half == 0:
-                    acc[n * NPAIR + j] = prod
-                else:
-                    sbufs[j % 2][...] = prod + acc[n * NPAIR + j]
-                    pick(sbufs[(j + 1) % 2], (n * NPAIR + j - 1) * (PAIR // LANES))
-            return carry
-
-        lax.fori_loop(0, n_steps, step, 0)
+        for j in range(n_pairs):
+            if j in points:
+                points[j]()
+            prod = lax.dot_general(h[hr, kc], w[pl.ds(j * PAIR, PAIR), kc], (((1,), (1,)), ((), ())),
+                                   preferred_element_type=jnp.float32)
+            if half == 0:
+                acc[j] = prod
+            else:
+                sbufs[j % 2][...] = prod + acc[j]
+                if j:
+                    pick(sbufs[(j + 1) % 2], (j - 1) * (PAIR // LANES))
         if half:
-            pick(sbufs[(NPAIR - 1) % 2], (n_steps * NPAIR - 1) * (PAIR // LANES))
+            pick(sbufs[(n_pairs - 1) % 2], (n_pairs - 1) * (PAIR // LANES))
 
     low = lax.broadcasted_iota(jnp.int32, (loc // 2, LANES), 1) < list_len
 
@@ -320,24 +305,29 @@
 
     r_a = pl.multiple_of((m // 2) * rows_half, rows_half)
     r_b = pl.multiple_of((1 - m // 2) * rows_half, rows_half)
-    run_phase(r_a, 0, (a0_0, a0_1, a0_2, a0_3))
+    own_valid.wait()
+    own_tgt.wait()
+    wait_w(0)
+    run_pass(r_a, 0, {4: a0_quarter, 8: a0_half, 12: a0_three})
     for b in near_sib:
         wait_ids(b)
         wait_h(b, halves[1])
+    a1_start()
     set_lists(r_a)
-    run_phase(r_a, 1, (a1_0, a1_1, a1_2, a1_3))
+    wait_w(1)
+    run_pass(r_a, 1, {4: a1_quarter, 12: a1_three})
     pack(r_a, (m // 2) * 8)
     backs = []
     for i, (zz, dv) in enumerate([(zp, 2), (zp, 3), (zp, 0), (zp, 1), (m, 2), (m, 1), (m, 3)]):
         backs.append(send_back(zz, lax.rem(v + dv, 4), i))
     for b in far_sib:
         wait_h(b, halves[0])
-    run_phase(r_b, 0, (None, b0_1, b0_2))
+    run_pass(r_b, 0, {8: b0_half})
     for b in far_sib:
         wait_ids(b)
         wait_h(b, halves[1])
     set_lists(r_b)
-    run_phase(r_b, 1, ())
+    run_pass(r_b, 1, {})
     pack(r_b, (1 - m // 2) * 8)
     for i, (zz, dv) in enumerate([(zf, dv) for zf in (far_far, far_near) for dv in (2, 3, 0, 1)]):
         backs.append(send_back(zz, lax.rem(v + dv, 4), 7 + i))
@@ -389,17 +379,18 @@
         loc, width = hidden.shape
         list_len = allowed_ids.shape[1]
         rows = 16 * loc
-        block = PAIR * NPAIR
-        w_rows = pl.cdiv(head_rows.shape[0], block) * block
+        w_rows = pl.cdiv(head_rows.shape[0], PAIR) * PAIR
         any_spec = pl.BlockSpec(memory_space=pl.ANY)
         vmem = pl.BlockSpec(memory_space=pltpu.VMEM)
         dma = pltpu.SemaphoreType.DMA
         p, lp = pl.pallas_call(
             head_kernel,
-            out_shape=(jax.ShapeDtypeStruct((loc, list_len), jnp.float32), jax.ShapeDtypeStruct((1, loc), jnp.float32)),
-            in_specs=[any_spec, any_spec, any_spec, vmem, vmem],
+            out_shape=(pltpu.VMEM((loc, list_len), jnp.float32), pltpu.VMEM((1, loc), jnp.float32)),
+            in_specs=[any_spec] * 5,
             out_specs=(vmem, vmem),
             scratch_shapes=[
+                pltpu.VMEM((loc, list_len), jnp.int32),
+                pltpu.VMEM((1, loc), jnp.int32),
                 pltpu.VMEM((w_rows, width), jnp.bfloat16),
                 pltpu.VMEM((rows, width), jnp.bfloat16),
                 pltpu.VMEM((w_rows // PAIR, rows // 2, PAIR), jnp.float32),
@@ -412,14 +403,14 @@
                 pltpu.VMEM((rows // 2, PAIR), jnp.float32),
                 pltpu.VMEM((rows // 2, PAIR), jnp.float32),
                 dma((pl.cdiv(head_rows.shape[0], W_ROWS), 2)),
-                dma, dma,
+                dma, dma, dma, dma,
                 dma((16, 4)),
                 dma((16,)),
                 dma((96,)),
                 dma((16,)),
                 dma((16,)),
             ],
-            compiler_params=pltpu.CompilerParams(collective_id=0, has_side_effects=True, vmem_limit_bytes=67043328),
+            compiler_params=pltpu.CompilerParams(collective_id=0, has_side_effects=True, vmem_limit_bytes=65500000),
         )(hidden, head_rows, allowed_ids, valid_mask, target_pos.reshape(1, loc))
         return p, lp.reshape(loc)
 

time: 55.7 us -> 51.2 us (0.919)
  Pallas kernels: 52.3 us -> 49.3 us
  local copies, waits for them, and re-layouts: 2.46 us -> 1.12 us
    pallas_call x1, Pallas kernels: 52.3 us -> 49.3 us  [local_step(): pl.pallas_call(head_kernel, out_shape=(pltpu.VMEM((loc, list_len), jnp.fl...]
    unnamed x2, local copies, waits for them, and re-layouts: 2.46 us -> 1.12 us
where the time goes in v3:
time: 51.2 us; the launch traced here: 51 us
  Pallas kernels  49.3 us (96%)
  local copies, waits for them, and re-layouts  1.12 us (2%)
  between operations  0.64 us (1%)
    pallas_call x1, Pallas kernels, local_step(): pl.pallas_call(head_kernel, out_shape=(pltpu.VMEM((loc, list_len), jnp.fl...  49.3 us
    unnamed x2, local copies, waits for them, and re-layouts  1.12 us

profile of v3, /device:TPU:0, one launch (start us, length us, event | category | flops | bytes accessed | tf_op | source)
XLA Modules:
  0.0 51.0 jit_solution(7877950080450387039)
XLA Ops:
  0.6 49.3 %shard_map.68 = (f32[32,64]{1,0:T(8,128)S(1)}, f32[1,32]{1,0:T(1,128)S(1)}) custom-call(bf16[32,3072]{1,0:T(8,128)(2,1)} %h_hbm.1, bf16[8016,3072]{1,0:T(8,128)(2,1)} %w_hbm.1, s32[32,64]{1,0:T(8,128)} %ids_hbm.1, s32[32,64]{1,0:T(8,128)} %valid_hbm.1, s32[1,32]{1,0:T(1,128)} %bitcast.3), custom_call_target="tpu_custom_call" | custom-call | tf_op jit(solution)/shard_map/pallas_call | solution.py:386
  49.9 0.6 %copy.9 = f32[32,64]{1,0:T(8,128)} copy(f32[32,64]{1,0:T(8,128)S(1)} %get-tuple-element.6) | data formatting | bytes 16384
  50.5 0.5 %copy.10 = f32[32]{0:T(128)} copy(f32[32]{0:T(128)S(1)} %bitcast.2) | data formatting | bytes 256

commit v4 on v3

--- a/solution.py
+++ b/solution.py
@@ -13,10 +13,11 @@
 LANES = 128
 W_ROWS = 1024
 ALL, INNER, OUTER = 0, 1, 2
+N_SENDS = 57
 
 
 def head_kernel(h_hbm, w_hbm, ids_hbm, valid_hbm, tgt_hbm, p_ref, lp_ref,
-                valid_ref, tgt_ref, w, h, acc, ids_all, lane, tile, picks, packed, back, sbuf0, sbuf1,
+                valid_ref, tgt_ref, ids_own, w, h, acc, ids_all, lane, tile, picks, packed, back, sbuf0, sbuf1,
                 w_sem, own_sem, own_ids_sem, valid_sem, tgt_sem, h_recv, ids_recv, send_sem, back_send, back_recv):
     m = lax.axis_index('model')
     v = lax.axis_index('vocab')
@@ -64,7 +65,7 @@
     own_h.start()
     own_valid = pltpu.make_async_copy(valid_hbm, valid_ref, valid_sem)
     own_tgt = pltpu.make_async_copy(tgt_hbm, tgt_ref, tgt_sem)
-    own_ids = pltpu.make_async_copy(ids_hbm, ids_all.at[row_block(me)], own_ids_sem)
+    own_ids = pltpu.make_async_copy(ids_hbm, ids_own, own_ids_sem)
     own_ids.start()
     own_valid.start()
     own_tgt.start()
@@ -72,8 +73,7 @@
         for i in range(n_chunks):
             w_copy(i, half).start(priority=1)
 
-    sent = {ALL: [], INNER: []}
-    n_sent = [0]
+    sent = {ALL: [], INNER: [], OUTER: []}
 
     def h_copy(k, blk, piece, dev):
         ref = h.at[row_block(blk), pl.ds(piece[0] * quarter, piece[1] * quarter)]
@@ -81,14 +81,15 @@
                                             device_id=dev, device_id_type=MESH)
 
     def ids_copy(k, blk, dev):
-        ref = ids_all.at[row_block(blk)]
+        ref = ids_all.at[blk]
         return pltpu.make_async_remote_copy(ref, ref, send_sem.at[k], ids_recv.at[blk],
                                             device_id=dev, device_id_type=MESH)
 
     def start(make, who):
-        make(n_sent[0]).start()
-        sent[who].append(functools.partial(make, n_sent[0]))
-        n_sent[0] += 1
+        i = len(sent[who])
+        k = i if who == ALL else N_SENDS - 1 - i
+        make(k).start()
+        sent[who].append(functools.partial(make, k))
 
     def send_h(blk, piece, dev, who=0):
         start(lambda k: h_copy(k, blk, piece, dev), who)
@@ -112,8 +113,9 @@
     quarters = tuple((q, 1) for q in range(4))
     halves = ((0, 2), (2, 2))
 
+    own_ids.wait()
+    ids_all[me] = jnp.concatenate([ids_own[: loc // 2, :], ids_own[loc // 2:, :]], axis=1)
     own_h.wait()
-    own_ids.wait()
     pl.semaphore_wait(barrier, 3 + inner_n)
 
     send_h(me, quarters[0], dev_y)
@@ -174,7 +176,6 @@
             wait_ids(b)
             send_ids(b, dev_sib, who)
 
-    sent[OUTER] = []
     outer = inner_n == 0
 
     pl.when(inner)(lambda: far(b_fn, 0))
@@ -256,12 +257,16 @@
 
     picks[...] = jnp.zeros_like(picks)
 
-    def set_lists(r0):
-        off = ids_all[pl.ds(r0, rows_half), :] - me * shard_len
-        off = jnp.concatenate([off, off], axis=1)
-        lane[...] = jnp.bitwise_and(off, LANES - 1)
-        good = jnp.logical_and(off >= 0, off < shard_len)
-        tile[...] = jnp.where(good, lax.shift_right_arithmetic(off, 7), 1 << 20)
+    low = lax.broadcasted_iota(jnp.int32, (loc // 2, LANES), 1) < list_len
+
+    def set_lists(b0):
+        for i in range(8):
+            off = ids_all[b0 + i] - me * shard_len
+            turned = pltpu.roll(off, LANES - list_len, 1)
+            for at, rows in ((0, jnp.where(low, off, turned)), (loc // 2, jnp.where(low, turned, off))):
+                good = jnp.logical_and(rows >= 0, rows < shard_len)
+                lane[i * loc + at:i * loc + at + loc // 2, :] = jnp.bitwise_and(rows, LANES - 1)
+                tile[i * loc + at:i * loc + at + loc // 2, :] = jnp.where(good, lax.shift_right_arithmetic(rows, 7), 1 << 20)
 
     sbufs = (sbuf0, sbuf1)
     n_pairs = w.shape[0] // PAIR
@@ -289,7 +294,6 @@
         if half:
             pick(sbufs[(n_pairs - 1) % 2], (n_pairs - 1) * (PAIR // LANES))
 
-    low = lax.broadcasted_iota(jnp.int32, (loc // 2, LANES), 1) < list_len
 
     def pack(r0, p0):
         for i in range(8):
@@ -313,7 +317,7 @@
         wait_ids(b)
         wait_h(b, halves[1])
     a1_start()
-    set_lists(r_a)
+    set_lists((m // 2) * 8)
     wait_w(1)
     run_pass(r_a, 1, {4: a1_quarter, 12: a1_three})
     pack(r_a, (m // 2) * 8)
@@ -326,7 +330,7 @@
     for b in far_sib:
         wait_ids(b)
         wait_h(b, halves[1])
-    set_lists(r_b)
+    set_lists((1 - m // 2) * 8)
     run_pass(r_b, 1, {})
     pack(r_b, (1 - m // 2) * 8)
     for i, (zz, dv) in enumerate([(zf, dv) for zf in (far_far, far_near) for dv in (2, 3, 0, 1)]):
@@ -353,6 +357,7 @@
     hit = lax.broadcasted_iota(jnp.int32, (loc, list_len), 1) == tgt_col
     picked = jnp.sum(jnp.where(hit, scores, 0.0), axis=1, keepdims=True)
     lp_ref[...] = jnp.sum(jnp.where(eye, picked - log_norm, 0.0), axis=0, keepdims=True)
+    assert len(sent[ALL]) + max(len(sent[INNER]), len(sent[OUTER])) == N_SENDS
     for make in sent[ALL]:
         make().wait_send()
 
@@ -391,10 +396,11 @@
             scratch_shapes=[
                 pltpu.VMEM((loc, list_len), jnp.int32),
                 pltpu.VMEM((1, loc), jnp.int32),
+                pltpu.VMEM((loc, list_len), jnp.int32),
                 pltpu.VMEM((w_rows, width), jnp.bfloat16),
                 pltpu.VMEM((rows, width), jnp.bfloat16),
                 pltpu.VMEM((w_rows // PAIR, rows // 2, PAIR), jnp.float32),
-                pltpu.VMEM((rows, list_len), jnp.int32),
+                pltpu.VMEM((16, loc // 2, LANES), jnp.int32),
                 pltpu.VMEM((rows // 2, LANES), jnp.int32),
                 pltpu.VMEM((rows // 2, LANES), jnp.int32),
                 pltpu.VMEM((rows, LANES), jnp.float32),
@@ -406,7 +412,7 @@
                 dma, dma, dma, dma,
                 dma((16, 4)),
                 dma((16,)),
-                dma((96,)),
+                dma((N_SENDS,)),
                 dma((16,)),
                 dma((16,)),
             ],

time: 51.2 us -> 50.8 us (level)
  no operation moved by 1% of the time
where the time goes in v4:
time: 50.8 us; the launch traced here: 50.7 us
  Pallas kernels  48.9 us (96%)
  local copies, waits for them, and re-layouts  1.12 us (2%)
  between operations  0.64 us (1%)
    pallas_call x1, Pallas kernels, local_step(): pl.pallas_call(head_kernel, out_shape=(pltpu.VMEM((loc, list_len), jnp.fl...  48.9 us
    unnamed x2, local copies, waits for them, and re-layouts  1.12 us

profile of v4, /device:TPU:0, one launch (start us, length us, event | category | flops | bytes accessed | tf_op | source)
XLA Modules:
  0.0 50.7 jit_solution(14327989793023331984)
XLA Ops:
  0.6 48.9 %shard_map.68 = (f32[32,64]{1,0:T(8,128)S(1)}, f32[1,32]{1,0:T(1,128)S(1)}) custom-call(bf16[32,3072]{1,0:T(8,128)(2,1)} %h_hbm.1, bf16[8016,3072]{1,0:T(8,128)(2,1)} %w_hbm.1, s32[32,64]{1,0:T(8,128)} %ids_hbm.1, s32[32,64]{1,0:T(8,128)} %valid_hbm.1, s32[1,32]{1,0:T(1,128)} %bitcast.3), custom_call_target="tpu_custom_call" | custom-call | tf_op jit(solution)/shard_map/pallas_call | solution.py:391
  49.5 0.6 %copy.9 = f32[32,64]{1,0:T(8,128)} copy(f32[32,64]{1,0:T(8,128)S(1)} %get-tuple-element.6) | data formatting | bytes 16384
  50.1 0.5 %copy.10 = f32[32]{0:T(128)} copy(f32[32]{0:T(128)S(1)} %bitcast.2) | data formatting | bytes 256
